TPU v7x, 512 devices: a whole 4x8x8 slice. The times are simulated.
512 devices in a mesh: row: 16 (over z, core), col: 32 (over x, y).
Axes of the slice: x: 4, y: 8, z: 8, core: 2. Of those that a mesh axis runs over, the one named last changes fastest.
Arguments:
- gram: bfloat16 [2, 16, 384, 1, 32, 384], P(None, 'row', None, None, 'col'), may hold values from -1 to 20, as said below
Outputs:
- swept: float32 [2, 16, 384, 1, 32, 384], P(None, 'row', None, None, 'col')
Inputs may be any that keep to these rules, and one draw needn't show every extreme that they name: gram is symmetric and positive definite.
All inputs are finite; a program needn't handle non-finite values.
Results may differ from a plain program's by a relative error of at most 0.0003.
Values sent between devices are 32-bit elements; how exact they have to be, the bound alone decides.
A program may use at most 64 MiB of HBM per device.

v0:
```python
import jax
import jax.numpy as jnp
from jax import lax
from jax.sharding import Mesh
from jax.sharding import PartitionSpec as P

PANELS = 2
COL = ("col_0", "col_1")


def from_root(array, axes, root):
    array = jnp.where(lax.axis_index(axes) == root, array, jnp.zeros_like(array))
    for axis in axes:
        array = lax.psum(array, axis)
    return array


def picked(array, axis, root):
    return lax.dynamic_index_in_dim(lax.all_gather(array, axis), root, 0, keepdims=False)


def solve_pivot(pivot_tile, right_side):
    factor = jnp.linalg.cholesky(pivot_tile)
    return jax.scipy.linalg.cho_solve((factor, True), right_side)


def skip_pivot(pivot_tile, right_side):
    return jnp.zeros_like(right_side)


def on_device(gram):
    row_count = lax.axis_size("row")
    col_count = lax.axis_size(COL)
    here_row = lax.axis_index("row")
    here_col = lax.axis_index(COL)
    row_tiles = gram.shape[0]
    breadth = gram.shape[2]
    col_tiles = gram.shape[3]
    matrix = gram.astype(jnp.float32).reshape(row_tiles * breadth, col_tiles * breadth)
    identity = jnp.eye(breadth, dtype=jnp.float32)
    highest = lax.Precision.HIGHEST
    for number in range(PANELS):
        root_row = number % row_count
        tile_row = number // row_count
        root_col = number % col_count
        tile_col = number // col_count
        row_lower = tile_row * breadth
        col_lower = tile_col * breadth
        on_row = here_row == root_row
        on_col = here_col == root_col
        own_column = matrix
        column = from_root(own_column, COL, root_col)
        pivot_tile = column[row_lower : row_lower + breadth]
        row_part = matrix[row_lower : row_lower + breadth]
        right_side = row_part.at[:, col_lower : col_lower + breadth].set(
            jnp.where(on_col, identity, row_part)
        )
        solved = lax.cond(on_row, solve_pivot, skip_pivot, pivot_tile, right_side)
        solved = picked(solved, "row", root_row)
        shifted = solved.at[:, col_lower : col_lower + breadth].add(
            jnp.where(on_col, identity, 0.0)
        )
        matrix = matrix - jnp.dot(
            column, shifted, precision=highest, preferred_element_type=jnp.float32
        )
        kept_rows = matrix[row_lower : row_lower + breadth]
        matrix = matrix.at[row_lower : row_lower + breadth].set(
            jnp.where(on_row, solved, kept_rows)
        )
    return matrix.reshape(gram.shape)


def solution(mesh):
    torus = Mesh(mesh.devices.reshape(mesh.shape["row"], 4, 8), ("row", "col_0", "col_1"))
    placed = (P(None, "row", None, None, COL, None),)
    return jax.shard_map(
        on_device,
        mesh=torus,
        in_specs=placed,
        out_specs=P(None, "row", None, None, COL, None),
        check_vma=False,
    )
```

profile of v0, /device:TPU:1, one launch (start us, length us, event | category | flops | bytes accessed | tf_op | source)
XLA Modules:
  0.0 649.4 jit_solution(17878175776577892573)
XLA Ops:
  6.5 2.0 copy_convert_fusion
  8.6 1.1 bitcast_select_fusion
  9.8 61.7 %all-reduce.6.cloned.1.call-done = f32[768,384]{1,0:T(8,128)} async-done(((f32[768,384]{1,0:T(8,128)}), f32[768,384]{1,0:T(8,128)}) %all-reduce.6.cloned.1.call-update) | async-done | bytes 1179664 | tf_op jit(solution)/shard_map/psum | solution.py:14
  71.5 1.2 compare_convert_fusion
  72.7 80.8 %all-reduce.8.cloned.1.call-done = f32[768,384]{1,0:T(8,128)} async-done(((f32[768,384]{1,0:T(8,128)}), f32[768,384]{1,0:T(8,128)}) %all-reduce.8.cloned.1.call-update) | async-done | bytes 1179664 | tf_op jit(solution)/shard_map/psum | solution.py:14
  153.5 3.9 conditional.2
  157.5 170.8 %all-gather.5.cloned.1.call-done = f32[6144,384]{1,0:T(8,128)} async-done(((f32[384,384]{1,0:T(8,128)}), f32[6144,384]{1,0:T(8,128)}) %all-gather.5.cloned.1.call-update) | async-done | bytes 9437200 | tf_op jit(solution)/shard_map/all_gather | solution.py:19
  328.3 3.8 convolution_subtract_fusion.13
  332.1 1.2 constant_dynamic-update-slice_fusion.6
  333.3 1.1 broadcast_select_fusion.2
  334.5 53.8 %all-reduce.10.cloned.1.call-done = f32[768,384]{1,0:T(8,128)} async-done(((f32[768,384]{1,0:T(8,128)}), f32[768,384]{1,0:T(8,128)}) %all-reduce.10.cloned.1.call-update) | async-done | bytes 1179664 | tf_op jit(solution)/shard_map/psum | solution.py:14
  389.2 80.9 %all-reduce.12.cloned.1.call-done = f32[768,384]{1,0:T(8,128)} async-done(((f32[768,384]{1,0:T(8,128)}), f32[768,384]{1,0:T(8,128)}) %all-reduce.12.cloned.1.call-update) | async-done | bytes 1179664 | tf_op jit(solution)/shard_map/psum | solution.py:14
  470.1 106.1 %conditional.3 = (f32[384,384]{1,0:T(8,128)S(1)}) conditional(s32[]{:T(128)} %convert_element_type.35, () %tuple.62, (f32[768,384]{1,0:T(8,128)}, pred[]{:T(512)}, f32[384,384]{1,0:T(8,128)}, f32[384,384]{1,0:T(8,128)S(1)}) %tuple.63), branch_computations={%region_12.15_spmd, %region_13.16_spmd} | conditional | flops 1084113280 | bytes 24120604 | solution.py:58
  470.3 1.6 copy.7
  472.7 1.3 copy.4
  474.9 11.7 %cholesky.261 = f32[128,128]{1,0:T(8,128)S(1)} custom-call(f32[128,128]{1,0:T(8,128)S(1)} %cholesky.318), custom_call_target="Cholesky" | custom-call | tf_op jit(solution)/shard_map/cond/branch_1_fun/jit(cholesky)/cholesky | solution.py:23
  486.7 9.8 %custom-call.25 = f32[1,128,128]{1,2,0:T(8,128)S(1)} custom-call(f32[1,128,128]{2,1,0:T(8,128)S(1)} %get-tuple-element.245), custom_call_target="InvertDiagBlocksLowerTriangular" | custom-call | tf_op jit(solution)/shard_map/cond/branch_1_fun/jit(cholesky)/cholesky | solution.py:23
  496.5 1.2 constant_dynamic-update-slice_fusion.5
  497.7 1.2 convolution_subtract_fusion.10
  498.9 11.7 %cholesky.280 = f32[128,128]{1,0:T(8,128)S(1)} custom-call(f32[128,128]{1,0:T(8,128)S(1)} %cholesky.322), custom_call_target="Cholesky" | custom-call | tf_op jit(solution)/shard_map/cond/branch_1_fun/jit(cholesky)/cholesky | solution.py:23
  512.5 10.0 %custom-call.26 = f32[1,128,128]{1,2,0:T(8,128)S(1)} custom-call(f32[1,128,128]{2,1,0:T(8,128)S(1)} %get-tuple-element.242), custom_call_target="InvertDiagBlocksLowerTriangular" | custom-call | tf_op jit(solution)/shard_map/cond/branch_1_fun/jit(cholesky)/cholesky | solution.py:23
  522.7 1.2 convolution_subtract_fusion.11
  523.9 11.7 %cholesky.299 = f32[128,128]{1,0:T(8,128)S(1)} custom-call(f32[128,128]{1,0:T(8,128)S(1)} %convolution_subtract_fusion.11), custom_call_target="Cholesky" | custom-call | tf_op jit(solution)/shard_map/cond/branch_1_fun/jit(cholesky)/cholesky | solution.py:23
  537.0 5.7 while.15
  537.6 1.3 bitcast_dynamic-update-slice_fusion.4
  539.5 1.3 bitcast_dynamic-update-slice_fusion.4
  541.4 1.3 bitcast_dynamic-update-slice_fusion.4
  542.7 29.5 %custom-call.27 = f32[3,128,128]{1,2,0:T(8,128)S(1)} custom-call(f32[3,128,128]{2,1,0:T(8,128)S(1)} %get-tuple-element.197), custom_call_target="InvertDiagBlocksLowerTriangular" | custom-call | tf_op jit(solution)/shard_map/cond/branch_1_fun/jit(_cho_solve)/triangular_solve | solution.py:24
  577.1 57.8 %all-gather.7.cloned.1.call-done = f32[6144,384]{1,0:T(8,128)} async-done(((f32[384,384]{1,0:T(8,128)}), f32[6144,384]{1,0:T(8,128)}) %all-gather.7.cloned.1.call-update) | async-done | bytes 9437200 | tf_op jit(solution)/shard_map/all_gather | solution.py:19
  634.9 3.9 convolution_subtract_fusion.12
  638.8 1.2 fusion.54
  639.9 2.2 copy.8
  (54 shorter events, 11.8 us)
Async XLA Ops:
  6.5 64.9 %all-reduce.6.cloned.1.call-start = ((), (), s32[]{:S(2)}) async-start(), calls=%async_computation | async-start | bytes 2359296 | tf_op jit(solution)/shard_map/psum | solution.py:14
  9.7 143.7 %all-reduce.8.cloned.1.call-start = ((), (), s32[]{:S(2)}) async-start(), calls=%async_computation.1 | async-start | bytes 2359296 | tf_op jit(solution)/shard_map/psum | solution.py:14
  71.5 256.8 %all-gather.5.cloned.1.call-start = ((), (), s32[]{:S(2)}) async-start(), calls=%async_computation.4 | async-start | bytes 10027008 | tf_op jit(solution)/shard_map/all_gather | solution.py:19
  157.4 230.8 %all-reduce.10.cloned.1.call-start = ((), (), s32[]{:S(2)}) async-start(), calls=%async_computation.2 | async-start | bytes 2359296 | tf_op jit(solution)/shard_map/psum | solution.py:14
  334.4 135.7 %all-reduce.12.cloned.1.call-start = ((), (), s32[]{:S(2)}) async-start(), calls=%async_computation.3 | async-start | bytes 2359296 | tf_op jit(solution)/shard_map/psum | solution.py:14
  388.3 246.6 %all-gather.7.cloned.1.call-start = ((), (), s32[]{:S(2)}) async-start(), calls=%async_computation.5 | async-start | bytes 10027008 | tf_op jit(solution)/shard_map/all_gather | solution.py:19
  474.1 0.8 copy-start.4
  522.7 49.5 %copy-start.2 = (f32[384,384]{1,0:T(8,128)S(1)}, f32[384,384]{1,0:T(8,128)}, u32[]{:S(2)}) copy-start(f32[384,384]{1,0:T(8,128)} %get-tuple-element.180) | copy-start | bytes 1769476 | tf_op jit(solution)/shard_map/cond
  576.2 0.8 copy-start
Sparse Core Ops, SparseCore 0:
  9.8 61.5 all-reduce.5
  73.8 79.5 all-reduce.7
  157.5 170.7 all-gather.4
  334.5 53.6 all-reduce.9
  390.4 79.6 all-reduce.11
  577.2 57.6 all-gather.6
where the time goes:
time: 660 us; the launch traced here: 649 us
  waiting for transfers between devices  506 us (77%)
  other arithmetic  94.6 us (14%)
  matrix products  14.9 us (2%)
  local copies, waits for them, and re-layouts  14.2 us (2%)
  between operations  14 us (2%)
    psum x4, waiting for transfers between devices, from_root(): array = lax.psum(array, axis)  277 us
    all_gather x2, waiting for transfers between devices, picked(): lax.all_gather(array, axis)  229 us
    another operation x10, other arithmetic, solve_pivot(): factor = jnp.linalg.cholesky(pivot_tile)  56.3 us
    another operation x5, other arithmetic, solve_pivot(): return jax.scipy.linalg.cho_solve((factor, True), right_side)  29.6 us
  transfers between devices with their start and end apart: 6, of which 6 were waited for; matrix products, arithmetic and copies ran while one was open for 0% of the time, Pallas kernels for 0%

commit v1 on v0

v1 whole, which is shorter than its diff:
```python
import functools

import jax
import jax.numpy as jnp
from jax import lax
from jax.experimental import pallas as pl
from jax.experimental.pallas import tpu as pltpu
from jax.sharding import Mesh
from jax.sharding import PartitionSpec as P

F32, BF16 = jnp.float32, jnp.bfloat16
MESH = pl.DeviceIdType.MESH
B = 128
NT = B // 8


def row_all(x, k):
    return jnp.broadcast_to(x[k : k + 1, :], (8, 128))


def row_pick(x, k):
    return jnp.take_along_axis(x, jnp.full((8, 128), k, jnp.int32), axis=0)


def lane_all(x, j):
    return jnp.broadcast_to(x[:, j : j + 1], (8, 128))


def tree(xs):
    xs = list(xs)
    while len(xs) > 1:
        xs = [sum(xs[i : i + 2][1:], xs[i]) for i in range(0, len(xs), 2)]
    return xs[0]


def inverse8(cols, sub):
    cols = list(cols)
    pivot = row_pick(cols[0], 0)
    for k in range(8):
        q = 1.0 / pivot
        if k < 7:
            cross = row_pick(cols[k], k + 1) * row_pick(cols[k + 1], k)
            pivot = row_pick(cols[k + 1], k + 1) - cross * q
        own = sub == k
        cq = cols[k] * q
        new = []
        for j in range(8):
            if j == k:
                new.append(jnp.where(own, q, -cq))
            else:
                r = row_pick(cols[j], k)
                new.append(jnp.where(own, r * q, cols[j] - cq * r))
        cols = new
    return cols


def inverse128(tiles):
    lane = lax.broadcasted_iota(jnp.int32, (8, 128), 1)
    sub = lax.broadcasted_iota(jnp.int32, (8, 128), 0)
    a = list(tiles)
    for s in range(NT):
        inv = inverse8([lane_all(a[s], 8 * s + j) for j in range(8)], sub)
        inside = (lane >= 8 * s) & (lane < 8 * s + 8)
        r = jnp.where(inside, jnp.where(lane - 8 * s == sub, 1.0, 0.0), a[s])
        w = tree([inv[k] * row_all(r, k) for k in range(8)])
        wr = [row_all(w, k) for k in range(8)]
        for t in range(NT):
            if t != s:
                acc = tree([lane_all(a[t], 8 * s + k) * wr[k] for k in range(8)])
                a[t] = jnp.where(inside, 0.0, a[t]) - acc
        a[s] = w
    return a


def split(x):
    hi = x.astype(BF16)
    return hi, (x - hi.astype(F32)).astype(BF16)


def dot(a, b):
    return jnp.dot(a, b, preferred_element_type=F32)


def dot3(a, b):
    return dot(a[0], b[0]) + (dot(a[0], b[1]) + dot(a[1], b[0]))


def eliminate(t, n):
    @pl.loop(0, n // B)
    def _(k):
        o = pl.multiple_of(k * B, B)
        tiles = [t[pl.ds(pl.multiple_of(o + 8 * i, 8), 8), pl.ds(o, B)] for i in range(NT)]
        inv = jnp.concatenate(inverse128(tiles), axis=0)
        for kk in range(n // B):

            @pl.when(k == kk)
            def _():
                own = slice(kk * B, kk * B + B)
                w = dot3(split(inv), split(t[own, kk * B + B :]))
                ws = split(w)
                for i in range(n // B):
                    if i != kk:
                        rows = slice(i * B, i * B + B)
                        t[rows, kk * B + B :] = t[rows, kk * B + B :] - dot3(split(t[rows, own]), ws)
                t[own, kk * B + B :] = w


def kernel(
    nz, nx, ny, tb, g_ref, out_ref, gf, cb, ob, t, sb,
    rc, ro, rg, rs, s_scat, s_y, s_x, s_xf, s_o, s_g, s_z, s_s,
):
    z, core, x, y = (lax.axis_index(a) for a in ("z", "core", "x", "y"))
    mate = 1 - core
    quarter = tb // nx
    step = quarter // 2
    s_step = tb // 4
    in_panel = (x == 0) & (y < 2)
    on_top = z == 0
    pending = []

    def put(cond, src, dst, send, recv, to):
        copy = pltpu.make_async_remote_copy(
            src_ref=src, dst_ref=dst, send_sem=send, recv_sem=recv, device_id=to, device_id_type=MESH
        )
        if cond is None:
            copy.start()
        else:
            pl.when(cond)(copy.start)
        pending.append((cond, copy))

    def arrived(cond, ref, recv):
        copy = pltpu.make_async_remote_copy(
            src_ref=ref, dst_ref=ref, send_sem=s_g, recv_sem=recv, device_id={"core": mate}, device_id_type=MESH
        )
        if cond is None:
            copy.wait_recv()
        else:
            pl.when(cond)(copy.wait_recv)

    def near(i, n):
        return lax.rem(i + n, n)

    for h in range(2):
        gf[h] = g_ref[h].astype(F32)
    for p in range(2):

        @pl.when((x == 0) & (y == p))
        def _():
            for h in range(2):
                cb[h, p, 0:quarter, :] = g_ref[h, 0:quarter, :].astype(F32)

    barrier = pltpu.get_barrier_semaphore()
    peers = [{"x": near(x + i, nx)} for i in range(1, nx)]
    peers += [{"y": near(y + 1, ny)}, {"y": near(y - 1, ny)}]
    peers += [{"z": near(z + 1, nz)}, {"z": near(z - 1, nz)}, {"core": mate}]
    for peer in peers:
        pl.semaphore_signal(barrier, inc=1, device_id=peer, device_id_type=MESH)
    pl.semaphore_wait(barrier, len(peers))

    put(on_top, gf.at[0], ob.at[2], s_g, rg, {"core": mate})

    def rows(q, k):
        return pl.ds(pl.multiple_of(q * quarter + k * step, 8), step)

    def to_mate(p, q, k):
        ref = cb.at[0, p, rows(q, k), :]
        put(on_top, ref, ob.at[p, rows(q, k), :], s_o.at[p, q, k], ro.at[p, q, k], {"core": mate})

    def also(gate, cond):
        return cond if gate is None else gate if cond is None else gate & cond

    def scatter(h, gate=None):
        for p in range(2):
            for k in range(2):
                for q in range(1, nx):
                    put(
                        also(gate, (x == 0) & (y == p)), gf.at[h, rows(q, k), :], cb.at[h, p, rows(q, k), :],
                        s_scat.at[h, p, k, q - 1], rc.at[h, p, q, k], {"x": q},
                    )

    def spread(h, gate=None):
        for k in range(2):
            for p in range(2):
                far = near(y - p, ny)
                ref = cb.at[h, p, rows(x, k), :]
                sem = rc.at[h, p, x, k]
                arrived(also(gate, (x > 0) | (y != p)), ref, sem)
                put(also(gate, far < ny // 2), ref, ref, s_y.at[h, p, k, 0], sem, {"y": near(y + 1, ny)})
                put(also(gate, (far == 0) | (far > ny // 2 + 1)), ref, ref, s_y.at[h, p, k, 1], sem, {"y": near(y - 1, ny)})
                put(gate, ref, ref, s_x.at[h, p, k, 0], sem, {"x": near(x + 1, nx)})
                put(gate, ref, ref, s_x.at[h, p, k, 1], sem, {"x": near(x - 1, nx)})
                if h == 0:
                    to_mate(p, x, k)
        for k in range(2):
            for p in range(2):
                for side in (-1, 1):
                    q = near(x + side, nx)
                    ref = cb.at[h, p, rows(q, k), :]
                    arrived(gate, ref, rc.at[h, p, q, k])
                    if side == (-1, 1)[p]:
                        put(gate, ref, ref, s_xf.at[h, p, k], rc.at[h, p, q, k], {"x": near(x - side, nx)})
                    if h == 0:
                        to_mate(p, q, k)
        for k in range(2):
            for p in range(2):
                q = near(x + 2, nx)
                arrived(gate, cb.at[h, p, rows(q, k), :], rc.at[h, p, q, k])
                if h == 0:
                    to_mate(p, q, k)

    scatter(0)
    spread(0)

    @pl.when(on_top)
    def _():
        arrived(None, ob.at[2], rg)
        for p in range(2):
            for q in range(nx):
                for k in range(2):
                    arrived(None, ob.at[p, rows(q, k), :], ro.at[p, q, k])
        r0 = lax.broadcasted_iota(jnp.int32, (tb, tb), 0)
        r1 = lax.broadcasted_iota(jnp.int32, (tb, tb), 1)
        eye = jnp.where(r0 == r1, 1.0, 0.0).astype(F32)
        mine = pl.ds(pl.multiple_of(core * tb, tb), tb)
        other = pl.ds(pl.multiple_of(mate * tb, tb), tb)
        for p in range(2):
            t[mine, p * tb : p * tb + tb] = cb[0, p]
            t[other, p * tb : p * tb + tb] = ob[p]
        t[mine, 2 * tb :] = jnp.where(in_panel, jnp.where(y == core, eye, 0.0), gf[0])
        t[other, 2 * tb :] = jnp.where(in_panel, jnp.where(y == mate, eye, 0.0), ob[2])
        eliminate(t, 2 * tb)
        for p in range(2):
            sb[p] = t[p * tb : p * tb + tb, 2 * tb :]

    scatter(1, z > 0)
    spread(1, z > 0)

    def s_rows(k):
        return pl.ds(k * s_step, s_step)

    for k in range(4):
        ref = sb.at[core, s_rows(k), :]
        sem = rs.at[core, k]
        arrived(z > 0, ref, sem)
        put(z < nz // 2, ref, ref, s_z.at[k, 0], sem, {"z": near(z + 1, nz)})
        put((z == 0) | (z > nz // 2 + 1), ref, ref, s_z.at[k, 1], sem, {"z": near(z - 1, nz)})
        put(z > 0, ref, ref, s_s.at[k], sem, {"core": mate})
    scatter(1, on_top)
    spread(1, on_top)
    for k in range(4):
        arrived(z > 0, sb.at[mate, s_rows(k), :], rs.at[mate, k])

    ss = [split(sb[p]) for p in range(2)]
    for h in range(2):
        total = jnp.where(in_panel, 0.0, gf[h])
        for p in range(2):
            c = cb[h, p].astype(BF16)
            total = total - (dot(c, ss[p][0]) + dot(c, ss[p][1]))
        out_ref[h] = total

    @pl.when(on_top)
    def _():
        out_ref[0] = sb[core]

    for cond, copy in pending:
        if cond is None:
            copy.wait_send()
        else:
            pl.when(cond)(copy.wait_send)


def on_device(nz, nx, ny, gram):
    tb = gram.shape[2]
    block = gram.reshape(2, tb, tb)
    dma = pltpu.SemaphoreType.DMA
    out = pl.pallas_call(
        functools.partial(kernel, nz, nx, ny, tb),
        out_shape=jax.ShapeDtypeStruct((2, tb, tb), F32),
        in_specs=[pl.BlockSpec(memory_space=pltpu.VMEM)],
        out_specs=pl.BlockSpec(memory_space=pltpu.VMEM),
        scratch_shapes=[
            pltpu.VMEM((2, tb, tb), F32),
            pltpu.VMEM((2, 2, tb, tb), F32),
            pltpu.VMEM((3, tb, tb), F32),
            pltpu.VMEM((2 * tb, 3 * tb), F32),
            pltpu.VMEM((2, tb, tb), F32),
            dma((2, 2, nx, 2)),
            dma((2, nx, 2)),
            dma(()),
            dma((2, 4)),
            dma((2, 2, 2, nx - 1)),
            dma((2, 2, 2, 2)),
            dma((2, 2, 2, 2)),
            dma((2, 2, 2)),
            dma((2, nx, 2)),
            dma(()),
            dma((4, 2)),
            dma((4,)),
        ],
        compiler_params=pltpu.CompilerParams(
            collective_id=0, has_side_effects=True, vmem_limit_bytes=48 << 20
        ),
    )(block)
    return out.reshape(gram.shape)


def solution(mesh):
    shape = (8, 2, 4, 8)
    torus = Mesh(mesh.devices.reshape(shape), ("z", "core", "x", "y"))
    spec = P(None, ("z", "core"), None, None, ("x", "y"), None)
    return jax.shard_map(
        functools.partial(on_device, shape[0], shape[2], shape[3]),
        mesh=torus,
        in_specs=(spec,),
        out_specs=spec,
        check_vma=False,
    )
```

time: 660 us -> 109 us (0.17)
  the two profiles are of different devices: /device:TPU:1 before, /device:TPU:40 now
where the time goes in v1:
time: 109 us
  Pallas kernels  106 us (97%)
  local copies, waits for them, and re-layouts  3.29 us (3%)
    pallas_call x1, Pallas kernels, on_device(): pl.pallas_call(functools.partial(kernel, nz, nx, ny, tb), out_shape=jax.S...  106 us
    reshape x1, local copies, waits for them, and re-layouts, on_device(): return out.reshape(gram.shape)  2.23 us

profile of v1, /device:TPU:40, one launch (start us, length us, event | category | flops | bytes accessed | tf_op | source)
XLA Modules:
  0.0 109.2 jit_solution(4941594702358076993)
XLA Ops:
  0.0 0.0 copy-start
  0.0 1.1 copy-done
  1.1 105.9 %shard_map.17 = f32[2,384,384]{2,1,0:T(8,128)S(1)} custom-call(bf16[2,384,384]{2,1,0:T(8,128)(2,1)S(1)} %bitcast.3), custom_call_target="tpu_custom_call" | custom-call | tf_op jit(solution)/shard_map/pallas_call | solution.py:276
  107.0 2.2 %copy.2 = f32[2,1,384,1,1,384]{5,4,3,2,1,0:T(1,128)} copy(f32[2,1,384,1,1,384]{5,2,0,4,3,1:T(8,128)S(1)} %bitcast.2) | data formatting | bytes 2359296 | tf_op jit(solution)/shard_map/reshape | solution.py:304
Async XLA Ops:
  0.0 1.1 copy-start

commit v2 on v1

v2 whole, which is shorter than its diff:
```python
import functools

import jax
import jax.numpy as jnp
from jax import lax
from jax.experimental import pallas as pl
from jax.experimental.pallas import tpu as pltpu
from jax.sharding import Mesh
from jax.sharding import PartitionSpec as P

F32, BF16 = jnp.float32, jnp.bfloat16
MESH = pl.DeviceIdType.MESH
B = 128
NT = B // 8


def row_all(x, k):
    return jnp.broadcast_to(x[k : k + 1, :], (8, 128))


def row_pick(x, k):
    return jnp.take_along_axis(x, jnp.full((8, 128), k, jnp.int32), axis=0)


def lane_all(x, j):
    return jnp.broadcast_to(x[:, j : j + 1], (8, 128))


def tree(xs):
    xs = list(xs)
    while len(xs) > 1:
        xs = [sum(xs[i : i + 2][1:], xs[i]) for i in range(0, len(xs), 2)]
    return xs[0]


def inverse8(cols, sub):
    cols = list(cols)
    pivot = row_pick(cols[0], 0)
    for k in range(8):
        q = 1.0 / pivot
        if k < 7:
            cross = row_pick(cols[k], k + 1) * row_pick(cols[k + 1], k)
            pivot = row_pick(cols[k + 1], k + 1) - cross * q
        own = sub == k
        cq = cols[k] * q
        new = []
        for j in range(8):
            if j == k:
                new.append(jnp.where(own, q, -cq))
            else:
                r = row_pick(cols[j], k)
                new.append(jnp.where(own, r * q, cols[j] - cq * r))
        cols = new
    return cols


def inverse128(tiles):
    lane = lax.broadcasted_iota(jnp.int32, (8, 128), 1)
    sub = lax.broadcasted_iota(jnp.int32, (8, 128), 0)
    a = list(tiles)
    for s in range(NT):
        inv = inverse8([lane_all(a[s], 8 * s + j) for j in range(8)], sub)
        inside = (lane >= 8 * s) & (lane < 8 * s + 8)
        r = jnp.where(inside, jnp.where(lane - 8 * s == sub, 1.0, 0.0), a[s])
        w = tree([inv[k] * row_all(r, k) for k in range(8)])
        wr = [row_all(w, k) for k in range(8)]
        for t in range(NT):
            if t != s:
                acc = tree([lane_all(a[t], 8 * s + k) * wr[k] for k in range(8)])
                a[t] = jnp.where(inside, 0.0, a[t]) - acc
        a[s] = w
    return a


def split(x):
    hi = x.astype(BF16)
    return hi, (x - hi.astype(F32)).astype(BF16)


def dot(a, b):
    return jnp.dot(a, b, preferred_element_type=F32)


def dot3(a, b):
    return dot(a[0], b[0]) + (dot(a[0], b[1]) + dot(a[1], b[0]))


def dot3_t(a, b):
    t = lambda u, v: lax.dot_general(u, v, (((1,), (1,)), ((), ())), preferred_element_type=F32)
    return t(a[0], b[0]) + (t(a[0], b[1]) + t(a[1], b[0]))


NB = 6
HALF = 3


def kernel(
    nz, nx, ny, tb, g_ref, out_ref, cb, rb, t11, fb, xs, dv, vb, lh, ll, xh, xl, yh, yl, zh, zl, vh, vl,
    rc, rm, rg, rt, rr, rf, s_scat, s_y, s_x, s_xf, s_m, s_g, s_t, s_rz, s_rm, sf,
):
    z, core, x, y = (lax.axis_index(a) for a in ("z", "core", "x", "y"))
    mate = 1 - core
    is0, is1 = core == 0, core == 1
    quarter = tb // nx
    top = z == 0
    root = is0 & top & (x == 0) & (y == 0)
    in_panel = (x == 0) & (y < 2)
    to_other = {"core": mate}
    pending = []

    def make(src, dst, send, recv, to):
        return pltpu.make_async_remote_copy(
            src_ref=src, dst_ref=dst, send_sem=send, recv_sem=recv, device_id=to, device_id_type=MESH
        )

    def put(cond, src, dst, send, recv, to):
        copy = make(src, dst, send, recv, to)
        pl.when(cond)(copy.start)
        pending.append((cond, copy))

    def arrived(cond, ref, recv):
        pl.when(cond)(make(ref, ref, s_t, recv, to_other).wait_recv)

    def near(i, n):
        return lax.rem(i + n, n)

    def rows(q):
        return pl.ds(pl.multiple_of(q * quarter, 8), quarter)

    for p in range(2):

        @pl.when((x == 0) & (y == p))
        def _():
            for h in range(2):
                cb[core, h, p] = g_ref[h].astype(F32)

    @pl.when(top)
    def _():
        rb[core] = g_ref[0].astype(F32)

    barrier = pltpu.get_barrier_semaphore()
    peers = [{"x": near(x + i, nx)} for i in range(1, nx)]
    for i in (-2, -1, 1, 2):
        peers += [{"y": near(y + i, ny)}, {"z": near(z + i, nz)}]
    peers += [to_other, {"y": y + 1 - 2 * lax.rem(y, 2), "core": mate}]
    for peer in peers:
        pl.semaphore_signal(barrier, inc=1, device_id=peer, device_id_type=MESH)
    pl.semaphore_wait(barrier, len(peers))

    def r_rows(c):
        return pl.ds(c * quarter, quarter)

    for c in range(4):
        ref = rb.at[1, r_rows(c), :]
        put(top & is1, ref, ref, s_rm.at[1, c], rr.at[1, c], to_other)
    put(is1 & top & (x == 0) & (y == 1), cb.at[1, 0, 1], t11, s_t, rt, {"core": 0, "y": 0})

    def needed(h):
        return z > 0 if h == 0 else z >= 0

    for h in range(2):
        for p in range(2):
            ref = cb.at[0, h, p]
            put(is0 & (x == 0) & (y == p) & needed(h), ref, ref, s_g.at[h], rg.at[h], to_other)

    def tree8(i, gate, late):
        hub = gate & ((i == 0) | (i == 2) | (i == 6))
        return [
            (hub, jnp.where(i == 0, 2, i - 1)),
            (hub, jnp.where(i == 0, 6, lax.rem(i + 1, 8))),
            (gate & (i == (2 if late else 3)), 4),
        ]

    for tile in range(2):
        for c in range(4):
            ref = rb.at[tile, r_rows(c), :]
            sem = rr.at[tile, c]
            arrived(is0 if tile else is0 & (z > 0), ref, sem)
            for n, (cond, to) in enumerate(tree8(z, is0, False)):
                put(cond, ref, ref, s_rz.at[tile, c, n], sem, {"z": to})
            put(is0 & (z > 0) if tile else is0, ref, ref, s_rm.at[tile, c] if tile == 0 else s_rz.at[tile, c, 3], sem, to_other)

    def scatter(r, h):
        for p in range(2):
            here = is1 & (x == 0) & (y == p) & needed(h)
            if r == 0:
                arrived(here, cb.at[0, h, p], rg.at[h])
            for q in range(1, nx):
                ref = cb.at[r, h, p, rows(q), :]
                put(here, ref, ref, s_scat.at[r, h, q - 1], rc.at[r, h, p, q], {"x": q})

    def to_mate(gate, r, h, p, q):
        if r == 0:
            ref = cb.at[0, h, p, rows(q), :]
            put(gate, ref, ref, s_m.at[h, p, q], rm.at[h, p, q], to_other)

    def spread(r, h):
        for p in range(2):
            gate = is1 & needed(h)
            src = (x == 0) & (y == p)
            far = near(y - p, ny)
            ref, sem = cb.at[r, h, p, rows(x), :], rc.at[r, h, p, x]
            arrived(gate & ((x > 0) | (y != p)), ref, sem)
            put(gate & (far < ny // 2), ref, ref, s_y.at[r, h, p, 0], sem, {"y": near(y + 1, ny)})
            put(gate & ((far == 0) | (far > ny // 2 + 1)), ref, ref, s_y.at[r, h, p, 1], sem, {"y": near(y - 1, ny)})
            for n, side in enumerate((1, -1)):
                to = near(x + side, nx)
                put(gate & ((to > 0) | (y != p)), ref, ref, s_x.at[r, h, p, n], sem, {"x": to})
            to_mate(gate & ((x > 0) | (y != p)), r, h, p, x)

    def gather(r, h):
        for p in range(2):
            gate = is1 & needed(h)
            get = gate & ((x > 0) | (y != p))
            for side in (-1, 1):
                q = near(x + side, nx)
                ref, sem = cb.at[r, h, p, rows(q), :], rc.at[r, h, p, q]
                arrived(get, ref, sem)
                if side == (-1, 1)[p]:
                    to = near(x - side, nx)
                    put(gate & ((to > 0) | (y != p)), ref, ref, s_xf.at[r, h, p], sem, {"x": to})
                to_mate(get, r, h, p, q)
        for p in range(2):
            get = is1 & needed(h) & ((x > 0) | (y != p))
            q = near(x + 2, nx)
            arrived(get, cb.at[r, h, p, rows(q), :], rc.at[r, h, p, q])
            to_mate(get, r, h, p, q)

    order = [(1, 0), (1, 1), (0, 0), (0, 1)]
    for r, h in order:
        scatter(r, h)
    for n, (r, h) in enumerate(order):
        spread(r, h)
        if n:
            gather(*order[n - 1])
    gather(*order[-1])

    items = [(k, i) for k in range(NB) for i in range(k, NB)]

    def item_sends(k, i):
        late = k >= NB - 2
        on_x = is0 & top & (y == 0)
        ways = [(on_x & (x == 0), {"x": 1}), (on_x & (x == 0), {"x": 3})]
        ways += [(on_x & (x == (0 if late else 1)), {"x": 2})]
        ways += [(c, {"y": to}) for c, to in tree8(y, is0 & top, late)]
        ways += [(c, {"z": to}) for c, to in tree8(z, is0, late)]
        ways += [(is0, to_other)]
        ref = fb.at[k, i]
        return [(c, make(ref, ref, sf.at[k, i, n], rf.at[k, i], to)) for n, (c, to) in enumerate(ways)]

    def relay(gate, k, i):
        @pl.when(gate)
        def _():
            make(fb.at[k, i], fb.at[k, i], s_t, rf.at[k, i], to_other).wait_recv()
            for cond, copy in item_sends(k, i):
                pl.when(cond)(copy.start)

    @pl.when(root)
    def _():
        @pl.loop(0, NB)
        def _(j):
            for jj in range(NB):

                @pl.when(j == jj)
                def _():
                    lo = jj * B
                    if jj == HALF:
                        make(t11, t11, s_t, rt, to_other).wait_recv()
                    acc = 0.0
                    if jj:
                        acc = dot3_t((lh[lo:, :lo], ll[lo:, :lo]), (xh[lo : lo + B, :lo], xl[lo : lo + B, :lo]))
                    if jj < HALF:
                        a = jnp.concatenate([rb[0, lo:, lo : lo + B], rb[1, :, lo : lo + B]], axis=0)
                    else:
                        a = t11[lo - tb :, lo - tb : lo - tb + B]
                    xs[lo:, :] = a - acc

            o = pl.multiple_of(j * B, B)
            tiles = [xs[pl.ds(pl.multiple_of(o + 8 * i, 8), 8), :] for i in range(NT)]
            inv = inverse128(tiles)
            for i in range(NT):
                dv[8 * i : 8 * i + 8, :] = inv[i]
            for jj in range(NB):

                @pl.when(j == jj)
                def _():
                    lo = jj * B
                    fb[jj, jj] = dv[...]
                    if jj < NB - 1:
                        xc = split(xs[lo + B :, :])
                        w = dot3(xc, split(dv[...]))
                        wc = split(w)
                        xh[lo + B :, lo : lo + B], xl[lo + B :, lo : lo + B] = xc
                        lh[lo + B :, lo : lo + B], ll[lo + B :, lo : lo + B] = wc
                        for i in range(jj + 1, NB):
                            fb[jj, i] = w[(i - jj - 1) * B : (i - jj) * B, :]
                    for i in range(jj, NB):
                        for cond, copy in item_sends(jj, i):
                            pl.when(cond)(copy.start)

    others = is0 & jnp.logical_not(root)
    hub = (z == 0) | (z == 2) | (z == 6)
    for k, i in items[:-1]:
        relay(others, k, i)
    relay(others & hub, *items[-1])

    for tile in range(2):
        for c in range(4):
            arrived(is1 & (z > 0) if tile else is1, rb.at[tile, r_rows(c), :], rr.at[tile, c])
    for h in range(2):
        for p in range(2):
            for q in range(nx):
                get = is0 & needed(h) & ((x > 0) | (y != p))
                arrived(get, cb.at[0, h, p, rows(q), :], rm.at[h, p, q])
    for k, i in items[:-1]:
        arrived(is1, fb.at[k, i], rf.at[k, i])

    def unit(shape, shift):
        r = lax.broadcasted_iota(jnp.int32, shape, 0)
        return jnp.where(r - lax.broadcasted_iota(jnp.int32, shape, 1) == shift, 1.0, 0.0).astype(F32)

    def update(lo, hi, first):
        for h in range(2):
            o = h * tb
            c = (vh[o : o + tb, lo:hi], vl[o : o + tb, lo:hi])
            w = (zh[lo:hi, :], zl[lo:hi, :])
            if first:
                keep = jnp.logical_not(in_panel | (top & (h == 0)))
                base = jnp.where(keep, g_ref[h].astype(F32), 0.0)
            else:
                base = out_ref[h]
            out_ref[h] = base - dot3(c, w)

    def solve(k):
        lo = k * B
        w = split(dot3(split(fb[k, k]), (yh[lo : lo + B, :], yl[lo : lo + B, :])))
        zh[lo : lo + B, :], zl[lo : lo + B, :] = w

    for k in range(NB):
        lo = k * B
        for j in range(k):
            lh[lo : lo + B, j * B : j * B + B], ll[lo : lo + B, j * B : j * B + B] = split(fb[j, k])
        p, off = k // HALF, k % HALF * B
        yk = jnp.where(in_panel, jnp.where(y == p, unit((B, tb), -off), 0.0), rb[p, off : off + B, :])
        if k:
            lk = (lh[lo : lo + B, :lo], ll[lo : lo + B, :lo])
            yk = yk - dot3(lk, (yh[:lo, :], yl[:lo, :]))
        yh[lo : lo + B, :], yl[lo : lo + B, :] = split(yk)
        for h in range(2):
            o = h * tb
            if h == 0:

                @pl.when(top)
                def _():
                    vb[...] = jnp.where(core == p, -unit((tb, B), off), 0.0)

                @pl.when(z > 0)
                def _():
                    vb[...] = cb[core, 0, p, :, off : off + B]

            vk = vb[...] if h == 0 else cb[core, h, p, :, off : off + B]
            if k:
                vk = vk - dot3_t((vh[o : o + tb, :lo], vl[o : o + tb, :lo]), lk)
            vh[o : o + tb, lo : lo + B], vl[o : o + tb, lo : lo + B] = split(vk)
        if k < NB - 1:
            solve(k)
    update(0, (NB - 1) * B, True)

    relay(others & jnp.logical_not(hub), *items[-1])
    arrived(is1, fb.at[items[-1][0], items[-1][1]], rf.at[items[-1][0], items[-1][1]])
    solve(NB - 1)
    update((NB - 1) * B, NB * B, False)

    for cond, copy in pending:
        pl.when(cond)(copy.wait_send)
    for k, i in items:
        for cond, copy in item_sends(k, i):
            pl.when(cond)(copy.wait_send)


def on_device(nz, nx, ny, gram):
    tb = gram.shape[2]
    block = gram.reshape(2, tb, tb)
    dma = pltpu.SemaphoreType.DMA
    n = 2 * tb
    wide = [pltpu.VMEM((n, n), BF16)]
    tall = [pltpu.VMEM((n, tb), BF16)]
    out = pl.pallas_call(
        functools.partial(kernel, nz, nx, ny, tb),
        out_shape=jax.ShapeDtypeStruct((2, tb, tb), F32),
        in_specs=[pl.BlockSpec(memory_space=pltpu.VMEM)],
        out_specs=pl.BlockSpec(memory_space=pltpu.VMEM),
        scratch_shapes=[
            pltpu.VMEM((2, 2, 2, tb, tb), F32),
            pltpu.VMEM((2, tb, tb), F32),
            pltpu.VMEM((tb, tb), F32),
            pltpu.VMEM((NB, NB, B, B), F32),
            pltpu.VMEM((n, B), F32),
            pltpu.VMEM((B, B), F32),
            pltpu.VMEM((tb, B), F32),
        ]
        + wide * 4 + tall * 4 + wide * 2
        + [
            dma((2, 2, 2, nx)),
            dma((2, 2, nx)),
            dma((2,)),
            dma(()),
            dma((2, 4)),
            dma((NB, NB)),
            dma((2, 2, nx - 1)),
            dma((2, 2, 2, 2)),
            dma((2, 2, 2, 2)),
            dma((2, 2, 2)),
            dma((2, 2, nx)),
            dma((2,)),
            dma(()),
            dma((2, 4, 4)),
            dma((2, 4)),
            dma((NB, NB, 10)),
        ],
        compiler_params=pltpu.CompilerParams(
            collective_id=0, has_side_effects=True, vmem_limit_bytes=48 << 20
        ),
    )(block)
    return out.reshape(gram.shape)


def solution(mesh):
    shape = (8, 2, 4, 8)
    torus = Mesh(mesh.devices.reshape(shape), ("z", "core", "x", "y"))
    spec = P(None, ("z", "core"), None, None, ("x", "y"), None)
    return jax.shard_map(
        functools.partial(on_device, shape[0], shape[2], shape[3]),
        mesh=torus,
        in_specs=(spec,),
        out_specs=spec,
        check_vma=False,
    )
```

time: 109 us -> 90.4 us (0.83)
  the two profiles are of different devices: /device:TPU:40 before, /device:TPU:105 now
where the time goes in v2:
time: 90.4 us; the launch traced here: 90.2 us
  Pallas kernels  86.9 us (96%)
  local copies, waits for them, and re-layouts  3.29 us (4%)
    pallas_call x1, Pallas kernels, on_device(): pl.pallas_call(functools.partial(kernel, nz, nx, ny, tb), out_shape=jax.S...  86.9 us
    reshape x1, local copies, waits for them, and re-layouts, on_device(): return out.reshape(gram.shape)  2.23 us

profile of v2, /device:TPU:105, one launch (start us, length us, event | category | flops | bytes accessed | tf_op | source)
XLA Modules:
  0.0 90.2 jit_solution(6496920629253152554)
XLA Ops:
  0.0 0.0 copy-start
  0.0 1.1 %copy-done = bf16[2,1,384,1,1,384]{5,2,4,3,1,0:T(8,128)(2,1)S(1)} copy-done((bf16[2,1,384,1,1,384]{5,2,4,3,1,0:T(8,128)(2,1)S(1)}, bf16[2,1,384,1,1,384]{5,2,4,3,1,0:T(8,128)(2,1)}, u32[]{:S(2)}) %copy-start) | copy-done | bytes 589848
  1.1 86.9 %shard_map.17 = f32[2,384,384]{2,1,0:T(8,128)S(1)} custom-call(bf16[2,384,384]{2,1,0:T(8,128)(2,1)S(1)} %bitcast.3), custom_call_target="tpu_custom_call" | custom-call | tf_op jit(solution)/shard_map/pallas_call | solution.py:388
  88.0 2.2 %copy.2 = f32[2,1,384,1,1,384]{5,4,3,2,1,0:T(1,128)} copy(f32[2,1,384,1,1,384]{5,2,0,4,3,1:T(8,128)S(1)} %bitcast.2) | data formatting | bytes 2359296 | tf_op jit(solution)/shard_map/reshape | solution.py:425
Async XLA Ops:
  0.0 1.1 %copy-start = (bf16[2,1,384,1,1,384]{5,2,4,3,1,0:T(8,128)(2,1)S(1)}, bf16[2,1,384,1,1,384]{5,2,4,3,1,0:T(8,128)(2,1)}, u32[]{:S(2)}) copy-start(bf16[2,1,384,1,1,384]{5,2,4,3,1,0:T(8,128)(2,1)} %param.1) | copy-start | bytes 1769476

commit v3 on v2

--- a/solution.py
+++ b/solution.py
@@ -92,11 +92,13 @@
 
 NB = 6
 HALF = 3
+CUT = 1
+SPAN = 1
 
 
 def kernel(
     nz, nx, ny, tb, g_ref, out_ref, cb, rb, t11, fb, xs, dv, vb, lh, ll, xh, xl, yh, yl, zh, zl, vh, vl,
-    rc, rm, rg, rt, rr, rf, s_scat, s_y, s_x, s_xf, s_m, s_g, s_t, s_rz, s_rm, sf,
+    rc, rm, rg, rt, rr, rf, s_scat, s_y, s_x, s_xf, s_m, s_g, s_t, s_r, sf,
 ):
     z, core, x, y = (lax.axis_index(a) for a in ("z", "core", "x", "y"))
     mate = 1 - core
@@ -124,8 +126,10 @@
     def near(i, n):
         return lax.rem(i + n, n)
 
-    def rows(q):
-        return pl.ds(pl.multiple_of(q * quarter, 8), quarter)
+    piece = quarter // CUT
+
+    def rows(q, k):
+        return pl.ds(pl.multiple_of(q * quarter + k * piece, 8), piece)
 
     for p in range(2):
 
@@ -147,116 +151,129 @@
         pl.semaphore_signal(barrier, inc=1, device_id=peer, device_id_type=MESH)
     pl.semaphore_wait(barrier, len(peers))
 
-    def r_rows(c):
-        return pl.ds(c * quarter, quarter)
-
-    for c in range(4):
-        ref = rb.at[1, r_rows(c), :]
-        put(top & is1, ref, ref, s_rm.at[1, c], rr.at[1, c], to_other)
-    put(is1 & top & (x == 0) & (y == 1), cb.at[1, 0, 1], t11, s_t, rt, {"core": 0, "y": 0})
-
-    def needed(h):
-        return z > 0 if h == 0 else z >= 0
-
-    for h in range(2):
-        for p in range(2):
-            ref = cb.at[0, h, p]
-            put(is0 & (x == 0) & (y == p) & needed(h), ref, ref, s_g.at[h], rg.at[h], to_other)
-
-    def tree8(i, gate, late):
+    def tree8(i, gate, last):
         hub = gate & ((i == 0) | (i == 2) | (i == 6))
         return [
             (hub, jnp.where(i == 0, 2, i - 1)),
             (hub, jnp.where(i == 0, 6, lax.rem(i + 1, 8))),
-            (gate & (i == (2 if late else 3)), 4),
+            (gate & last, 4),
         ]
 
-    for tile in range(2):
-        for c in range(4):
-            ref = rb.at[tile, r_rows(c), :]
-            sem = rr.at[tile, c]
-            arrived(is0 if tile else is0 & (z > 0), ref, sem)
-            for n, (cond, to) in enumerate(tree8(z, is0, False)):
-                put(cond, ref, ref, s_rz.at[tile, c, n], sem, {"z": to})
-            put(is0 & (z > 0) if tile else is0, ref, ref, s_rm.at[tile, c] if tile == 0 else s_rz.at[tile, c, 3], sem, to_other)
-
-    def scatter(r, h):
+    def r_rows(c):
+        return pl.ds(c * quarter, quarter)
+
+    def r_sends(c):
+        ref, sem = rb.at[core, r_rows(c), :], rr.at[core, c]
+        ways = [(cond, {"z": to}) for cond, to in tree8(z, z >= 0, (is0 & (z == 2)) | (is1 & (z == 6)))]
+        ways += [(z >= 0, to_other)]
+        return [(cond, make(ref, ref, s_r.at[c, n], sem, to)) for n, (cond, to) in enumerate(ways)]
+
+    def r_relay(gate):
+        @pl.when(gate)
+        def _():
+            for c in range(4):
+                ref = rb.at[core, r_rows(c), :]
+                pl.when(z > 0)(make(ref, ref, s_t, rr.at[core, c], to_other).wait_recv)
+                for cond, copy in r_sends(c):
+                    pl.when(cond)(copy.start)
+
+    put(is1 & top & (x == 0) & (y == 1), cb.at[1, 0, 1], t11, s_t, rt, {"core": 0, "y": 0})
+    for p in range(2):
+        ref = cb.at[0, 1, p]
+        put(is0 & top & (x == 0) & (y == p), ref, ref, s_g, rg, to_other)
+    r_relay(top)
+
+    busy = (z > 0) | is1
+
+    def part(n):
+        return jnp.where(top, 1 - n, core), jnp.where(top, 1, n)
+
+    def scatter(n):
+        r, h = part(n)
         for p in range(2):
-            here = is1 & (x == 0) & (y == p) & needed(h)
-            if r == 0:
-                arrived(here, cb.at[0, h, p], rg.at[h])
-            for q in range(1, nx):
-                ref = cb.at[r, h, p, rows(q), :]
-                put(here, ref, ref, s_scat.at[r, h, q - 1], rc.at[r, h, p, q], {"x": q})
-
-    def to_mate(gate, r, h, p, q):
-        if r == 0:
-            ref = cb.at[0, h, p, rows(q), :]
-            put(gate, ref, ref, s_m.at[h, p, q], rm.at[h, p, q], to_other)
-
-    def spread(r, h):
-        for p in range(2):
-            gate = is1 & needed(h)
-            src = (x == 0) & (y == p)
-            far = near(y - p, ny)
-            ref, sem = cb.at[r, h, p, rows(x), :], rc.at[r, h, p, x]
-            arrived(gate & ((x > 0) | (y != p)), ref, sem)
-            put(gate & (far < ny // 2), ref, ref, s_y.at[r, h, p, 0], sem, {"y": near(y + 1, ny)})
-            put(gate & ((far == 0) | (far > ny // 2 + 1)), ref, ref, s_y.at[r, h, p, 1], sem, {"y": near(y - 1, ny)})
-            for n, side in enumerate((1, -1)):
-                to = near(x + side, nx)
-                put(gate & ((to > 0) | (y != p)), ref, ref, s_x.at[r, h, p, n], sem, {"x": to})
-            to_mate(gate & ((x > 0) | (y != p)), r, h, p, x)
-
-    def gather(r, h):
-        for p in range(2):
-            gate = is1 & needed(h)
-            get = gate & ((x > 0) | (y != p))
-            for side in (-1, 1):
-                q = near(x + side, nx)
-                ref, sem = cb.at[r, h, p, rows(q), :], rc.at[r, h, p, q]
+            here = busy & (x == 0) & (y == p)
+            if n:
+                arrived(here & top, cb.at[0, 1, p], rg)
+            for k in range(CUT):
+                for q in (2, 1, 3):
+                    ref = cb.at[r, h, p, rows(q, k), :]
+                    put(here, ref, ref, s_scat.at[n, q - 1, k], rc.at[n, p, q, k], {"x": q})
+
+    def to_mate(gate, n, p, q, k):
+        if n:
+            ref = cb.at[0, 1, p, rows(q, k), :]
+            put(gate & top, ref, ref, s_m.at[p, q, k], rm.at[p, q, k], to_other)
+
+    def spread(n):
+        r, h = part(n)
+        for k in range(CUT):
+            for p in range(2):
+                get = busy & ((x > 0) | (y != p))
+                far = near(y - p, ny)
+                ref, sem = cb.at[r, h, p, rows(x, k), :], rc.at[n, p, x, k]
                 arrived(get, ref, sem)
-                if side == (-1, 1)[p]:
-                    to = near(x - side, nx)
-                    put(gate & ((to > 0) | (y != p)), ref, ref, s_xf.at[r, h, p], sem, {"x": to})
-                to_mate(get, r, h, p, q)
-        for p in range(2):
-            get = is1 & needed(h) & ((x > 0) | (y != p))
-            q = near(x + 2, nx)
-            arrived(get, cb.at[r, h, p, rows(q), :], rc.at[r, h, p, q])
-            to_mate(get, r, h, p, q)
-
-    order = [(1, 0), (1, 1), (0, 0), (0, 1)]
-    for r, h in order:
-        scatter(r, h)
-    for n, (r, h) in enumerate(order):
-        spread(r, h)
-        if n:
-            gather(*order[n - 1])
-    gather(*order[-1])
-
-    items = [(k, i) for k in range(NB) for i in range(k, NB)]
+                put(busy & (far < ny // 2), ref, ref, s_y.at[n, p, k, 0], sem, {"y": near(y + 1, ny)})
+                back = busy & ((far == 0) | (far > ny // 2 + 1))
+                put(back, ref, ref, s_y.at[n, p, k, 1], sem, {"y": near(y - 1, ny)})
+                for i, side in enumerate((1, -1)):
+                    to = near(x + side, nx)
+                    put(busy & ((to > 0) | (y != p)), ref, ref, s_x.at[n, p, k, i], sem, {"x": to})
+                to_mate(get, n, p, x, k)
+
+    def gather(n):
+        r, h = part(n)
+        for k in range(CUT):
+            for p in range(2):
+                get = busy & ((x > 0) | (y != p))
+                for side in (-1, 1):
+                    q = near(x + side, nx)
+                    ref, sem = cb.at[r, h, p, rows(q, k), :], rc.at[n, p, q, k]
+                    arrived(get, ref, sem)
+                    if side == (-1, 1)[p]:
+                        to = near(x - side, nx)
+                        put(busy & ((to > 0) | (y != p)), ref, ref, s_xf.at[n, p, k], sem, {"x": to})
+                    to_mate(get, n, p, q, k)
+
+    def gather_far(n):
+        r, h = part(n)
+        for k in range(CUT):
+            for p in range(2):
+                get = busy & ((x > 0) | (y != p))
+                q = near(x + 2, nx)
+                arrived(get, cb.at[r, h, p, rows(q, k), :], rc.at[n, p, q, k])
+                to_mate(get, n, p, q, k)
+
+    scatter(0)
+    scatter(1)
+
+    items = [(k, i) for k in range(NB) for i in range(k, NB, SPAN)]
+
+    def blocks(k, i):
+        return fb.at[k, i : min(i + SPAN, NB)]
 
     def item_sends(k, i):
         late = k >= NB - 2
         on_x = is0 & top & (y == 0)
         ways = [(on_x & (x == 0), {"x": 1}), (on_x & (x == 0), {"x": 3})]
         ways += [(on_x & (x == (0 if late else 1)), {"x": 2})]
-        ways += [(c, {"y": to}) for c, to in tree8(y, is0 & top, late)]
-        ways += [(c, {"z": to}) for c, to in tree8(z, is0, late)]
+        ways += [(c, {"y": to}) for c, to in tree8(y, is0 & top, y == (2 if late else 3))]
+        ways += [(c, {"z": to}) for c, to in tree8(z, is0, z == (2 if late else 3))]
         ways += [(is0, to_other)]
-        ref = fb.at[k, i]
+        ref = blocks(k, i)
         return [(c, make(ref, ref, sf.at[k, i, n], rf.at[k, i], to)) for n, (c, to) in enumerate(ways)]
 
     def relay(gate, k, i):
         @pl.when(gate)
         def _():
-            make(fb.at[k, i], fb.at[k, i], s_t, rf.at[k, i], to_other).wait_recv()
+            make(blocks(k, i), blocks(k, i), s_t, rf.at[k, i], to_other).wait_recv()
             for cond, copy in item_sends(k, i):
                 pl.when(cond)(copy.start)
 
     @pl.when(root)
     def _():
+        for c in range(4):
+            make(rb.at[1, r_rows(c), :], rb.at[1, r_rows(c), :], s_t, rr.at[1, c], to_other).wait_recv()
+
         @pl.loop(0, NB)
         def _(j):
             for jj in range(NB):
@@ -294,42 +311,50 @@
                         lh[lo + B :, lo : lo + B], ll[lo + B :, lo : lo + B] = wc
                         for i in range(jj + 1, NB):
                             fb[jj, i] = w[(i - jj - 1) * B : (i - jj) * B, :]
-                    for i in range(jj, NB):
+                    for i in range(jj, NB, SPAN):
                         for cond, copy in item_sends(jj, i):
                             pl.when(cond)(copy.start)
 
     others = is0 & jnp.logical_not(root)
     hub = (z == 0) | (z == 2) | (z == 6)
+
+    def step(k):
+        for i in range(k, NB, SPAN):
+            relay(others, k, i)
+
+    spoke = (z == 2) | (z == 6)
+    spread(0)
+    r_relay(spoke)
+    spread(1)
+    step(0)
+    gather(0)
+    step(1)
+    gather(1)
+    step(2)
+    step(3)
+    step(4)
+    r_relay(jnp.logical_not(spoke | top))
+    relay(others & hub, *items[-1])
+
+    for c in range(4):
+        arrived(jnp.logical_not(root), rb.at[mate, r_rows(c), :], rr.at[mate, c])
     for k, i in items[:-1]:
-        relay(others, k, i)
-    relay(others & hub, *items[-1])
-
-    for tile in range(2):
-        for c in range(4):
-            arrived(is1 & (z > 0) if tile else is1, rb.at[tile, r_rows(c), :], rr.at[tile, c])
-    for h in range(2):
-        for p in range(2):
-            for q in range(nx):
-                get = is0 & needed(h) & ((x > 0) | (y != p))
-                arrived(get, cb.at[0, h, p, rows(q), :], rm.at[h, p, q])
-    for k, i in items[:-1]:
-        arrived(is1, fb.at[k, i], rf.at[k, i])
+        arrived(is1, blocks(k, i), rf.at[k, i])
 
     def unit(shape, shift):
         r = lax.broadcasted_iota(jnp.int32, shape, 0)
         return jnp.where(r - lax.broadcasted_iota(jnp.int32, shape, 1) == shift, 1.0, 0.0).astype(F32)
 
-    def update(lo, hi, first):
-        for h in range(2):
-            o = h * tb
-            c = (vh[o : o + tb, lo:hi], vl[o : o + tb, lo:hi])
-            w = (zh[lo:hi, :], zl[lo:hi, :])
-            if first:
-                keep = jnp.logical_not(in_panel | (top & (h == 0)))
-                base = jnp.where(keep, g_ref[h].astype(F32), 0.0)
-            else:
-                base = out_ref[h]
-            out_ref[h] = base - dot3(c, w)
+    def update(h, lo, hi, first):
+        o = h * tb
+        c = (vh[o : o + tb, lo:hi], vl[o : o + tb, lo:hi])
+        w = (zh[lo:hi, :], zl[lo:hi, :])
+        if first:
+            keep = jnp.logical_not(in_panel | (top & (h == 0)))
+            base = jnp.where(keep, g_ref[h].astype(F32), 0.0)
+        else:
+            base = out_ref[h]
+        out_ref[h] = base - dot3(c, w)
 
     def solve(k):
         lo = k * B
@@ -346,8 +371,14 @@
             lk = (lh[lo : lo + B, :lo], ll[lo : lo + B, :lo])
             yk = yk - dot3(lk, (yh[:lo, :], yl[:lo, :]))
         yh[lo : lo + B, :], yl[lo : lo + B, :] = split(yk)
-        for h in range(2):
-            o = h * tb
+        if k < NB - 1:
+            solve(k)
+
+    def columns(h):
+        o = h * tb
+        for k in range(NB):
+            lo = k * B
+            p, off = k // HALF, k % HALF * B
             if h == 0:
 
                 @pl.when(top)
@@ -360,21 +391,31 @@
 
             vk = vb[...] if h == 0 else cb[core, h, p, :, off : off + B]
             if k:
+                lk = (lh[lo : lo + B, :lo], ll[lo : lo + B, :lo])
                 vk = vk - dot3_t((vh[o : o + tb, :lo], vl[o : o + tb, :lo]), lk)
             vh[o : o + tb, lo : lo + B], vl[o : o + tb, lo : lo + B] = split(vk)
-        if k < NB - 1:
-            solve(k)
-    update(0, (NB - 1) * B, True)
+        update(h, 0, (NB - 1) * B, True)
+
+    gather_far(0)
+    columns(0)
+    gather_far(1)
+    for p in range(2):
+        for q in range(nx):
+            for k in range(CUT):
+                get = is0 & top & ((x > 0) | (y != p))
+                arrived(get, cb.at[0, 1, p, rows(q, k), :], rm.at[p, q, k])
+    columns(1)
 
     relay(others & jnp.logical_not(hub), *items[-1])
-    arrived(is1, fb.at[items[-1][0], items[-1][1]], rf.at[items[-1][0], items[-1][1]])
+    arrived(is1, blocks(*items[-1]), rf.at[NB - 1, NB - 1])
     solve(NB - 1)
-    update((NB - 1) * B, NB * B, False)
+    for h in range(2):
+        update(h, (NB - 1) * B, NB * B, False)
 
     for cond, copy in pending:
         pl.when(cond)(copy.wait_send)
-    for k, i in items:
-        for cond, copy in item_sends(k, i):
+    for copies in [r_sends(c) for c in range(4)] + [item_sends(k, i) for k, i in items]:
+        for cond, copy in copies:
             pl.when(cond)(copy.wait_send)
 
 
@@ -401,21 +442,20 @@
         ]
         + wide * 4 + tall * 4 + wide * 2
         + [
-            dma((2, 2, 2, nx)),
-            dma((2, 2, nx)),
-            dma((2,)),
+            dma((2, 2, nx, CUT)),
+            dma((2, nx, CUT)),
+            dma(()),
             dma(()),
             dma((2, 4)),
             dma((NB, NB)),
-            dma((2, 2, nx - 1)),
-            dma((2, 2, 2, 2)),
-            dma((2, 2, 2, 2)),
-            dma((2, 2, 2)),
-            dma((2, 2, nx)),
-            dma((2,)),
+            dma((2, nx - 1, CUT)),
+            dma((2, 2, CUT, 2)),
+            dma((2, 2, CUT, 2)),
+            dma((2, 2, CUT)),
+            dma((2, nx, CUT)),
             dma(()),
-            dma((2, 4, 4)),
-            dma((2, 4)),
+            dma(()),
+            dma((4, 4)),
             dma((NB, NB, 10)),
         ],
         compiler_params=pltpu.CompilerParams(

time: 90.4 us -> 86.3 us (0.955)
  the two profiles are of different devices: /device:TPU:105 before, /device:TPU:299 now
where the time goes in v3:
time: 86.3 us; the launch traced here: 86.2 us
  Pallas kernels  82.9 us (96%)
  local copies, waits for them, and re-layouts  3.29 us (4%)
    pallas_call x1, Pallas kernels, on_device(): pl.pallas_call(functools.partial(kernel, nz, nx, ny, tb), out_shape=jax.S...  82.9 us
    reshape x1, local copies, waits for them, and re-layouts, on_device(): return out.reshape(gram.shape)  2.23 us

profile of v3, /device:TPU:299, one launch (start us, length us, event | category | flops | bytes accessed | tf_op | source)
XLA Modules:
  0.0 86.2 jit_solution(18206378814812491786)
XLA Ops:
  0.0 0.0 copy-start
  0.0 1.1 %copy-done = bf16[2,1,384,1,1,384]{5,2,4,3,1,0:T(8,128)(2,1)S(1)} copy-done((bf16[2,1,384,1,1,384]{5,2,4,3,1,0:T(8,128)(2,1)S(1)}, bf16[2,1,384,1,1,384]{5,2,4,3,1,0:T(8,128)(2,1)}, u32[]{:S(2)}) %copy-start) | copy-done | bytes 589848
  1.1 82.9 %shard_map.17 = f32[2,384,384]{2,1,0:T(8,128)S(1)} custom-call(bf16[2,384,384]{2,1,0:T(8,128)(2,1)S(1)} %bitcast.3), custom_call_target="tpu_custom_call" | custom-call | tf_op jit(solution)/shard_map/pallas_call | solution.py:429
  83.9 2.2 %copy.2 = f32[2,1,384,1,1,384]{5,4,3,2,1,0:T(1,128)} copy(f32[2,1,384,1,1,384]{5,2,0,4,3,1:T(8,128)S(1)} %bitcast.2) | data formatting | bytes 2359296 | tf_op jit(solution)/shard_map/reshape | solution.py:465
Async XLA Ops:
  0.0 1.1 %copy-start = (bf16[2,1,384,1,1,384]{5,2,4,3,1,0:T(8,128)(2,1)S(1)}, bf16[2,1,384,1,1,384]{5,2,4,3,1,0:T(8,128)(2,1)}, u32[]{:S(2)}) copy-start(bf16[2,1,384,1,1,384]{5,2,4,3,1,0:T(8,128)(2,1)} %param.1) | copy-start | bytes 1769476

commit v4 on v3

--- a/solution.py
+++ b/solution.py
@@ -253,11 +253,12 @@
 
     def item_sends(k, i):
         late = k >= NB - 2
+        via = 2 if items.index((k, i)) % 2 else 6
         on_x = is0 & top & (y == 0)
         ways = [(on_x & (x == 0), {"x": 1}), (on_x & (x == 0), {"x": 3})]
         ways += [(on_x & (x == (0 if late else 1)), {"x": 2})]
-        ways += [(c, {"y": to}) for c, to in tree8(y, is0 & top, y == (2 if late else 3))]
-        ways += [(c, {"z": to}) for c, to in tree8(z, is0, z == (2 if late else 3))]
+        ways += [(c, {"y": to}) for c, to in tree8(y, is0 & top, y == via)]
+        ways += [(c, {"z": to}) for c, to in tree8(z, is0, z == via)]
         ways += [(is0, to_other)]
         ref = blocks(k, i)
         return [(c, make(ref, ref, sf.at[k, i, n], rf.at[k, i], to)) for n, (c, to) in enumerate(ways)]

time: 86.3 us -> 91.8 us (1.064)
  Pallas kernels: 82.9 us -> 88.3 us
    pallas_call x1, Pallas kernels: 82.9 us -> 88.3 us  [on_device(): pl.pallas_call(functools.partial(kernel, nz, nx, ny, tb), out_shape=jax.S...]
where the time goes in v4:
time: 91.8 us; the launch traced here: 91.7 us
  Pallas kernels  88.3 us (96%)
  local copies, waits for them, and re-layouts  3.29 us (4%)
    pallas_call x1, Pallas kernels, on_device(): pl.pallas_call(functools.partial(kernel, nz, nx, ny, tb), out_shape=jax.S...  88.3 us
    reshape x1, local copies, waits for them, and re-layouts, on_device(): return out.reshape(gram.shape)  2.23 us

profile of v4, /device:TPU:299, one launch (start us, length us, event | category | flops | bytes accessed | tf_op | source)
XLA Modules:
  0.0 91.7 jit_solution(12611920528167205033)
XLA Ops:
  0.0 0.0 copy-start
  0.0 1.1 %copy-done = bf16[2,1,384,1,1,384]{5,2,4,3,1,0:T(8,128)(2,1)S(1)} copy-done((bf16[2,1,384,1,1,384]{5,2,4,3,1,0:T(8,128)(2,1)S(1)}, bf16[2,1,384,1,1,384]{5,2,4,3,1,0:T(8,128)(2,1)}, u32[]{:S(2)}) %copy-start) | copy-done | bytes 589848
  1.1 88.3 %shard_map.17 = f32[2,384,384]{2,1,0:T(8,128)S(1)} custom-call(bf16[2,384,384]{2,1,0:T(8,128)(2,1)S(1)} %bitcast.3), custom_call_target="tpu_custom_call" | custom-call | tf_op jit(solution)/shard_map/pallas_call | solution.py:430
  89.4 2.2 %copy.2 = f32[2,1,384,1,1,384]{5,4,3,2,1,0:T(1,128)} copy(f32[2,1,384,1,1,384]{5,2,0,4,3,1:T(8,128)S(1)} %bitcast.2) | data formatting | bytes 2359296 | tf_op jit(solution)/shard_map/reshape | solution.py:466
Async XLA Ops:
  0.0 1.1 %copy-start = (bf16[2,1,384,1,1,384]{5,2,4,3,1,0:T(8,128)(2,1)S(1)}, bf16[2,1,384,1,1,384]{5,2,4,3,1,0:T(8,128)(2,1)}, u32[]{:S(2)}) copy-start(bf16[2,1,384,1,1,384]{5,2,4,3,1,0:T(8,128)(2,1)} %param.1) | copy-start | bytes 1769476

commit v5 on v3

--- a/solution.py
+++ b/solution.py
@@ -323,8 +323,10 @@
             relay(others, k, i)
 
     spoke = (z == 2) | (z == 6)
+    distant = (y > 2) & (y < 7)
+    r_relay(spoke & distant)
     spread(0)
-    r_relay(spoke)
+    r_relay(spoke & jnp.logical_not(distant))
     spread(1)
     step(0)
     gather(0)

time: 86.3 us -> 81.7 us (0.947)
  Pallas kernels: 82.9 us -> 78.2 us
    pallas_call x1, Pallas kernels: 82.9 us -> 78.2 us  [on_device(): pl.pallas_call(functools.partial(kernel, nz, nx, ny, tb), out_shape=jax.S...]
where the time goes in v5:
time: 81.7 us; the launch traced here: 81.5 us
  Pallas kernels  78.2 us (96%)
  local copies, waits for them, and re-layouts  3.29 us (4%)
    pallas_call x1, Pallas kernels, on_device(): pl.pallas_call(functools.partial(kernel, nz, nx, ny, tb), out_shape=jax.S...  78.2 us
    reshape x1, local copies, waits for them, and re-layouts, on_device(): return out.reshape(gram.shape)  2.23 us

profile of v5, /device:TPU:299, one launch (start us, length us, event | category | flops | bytes accessed | tf_op | source)
XLA Modules:
  0.0 81.5 jit_solution(14799885948043957709)
XLA Ops:
  0.0 0.0 copy-start
  0.0 1.1 %copy-done = bf16[2,1,384,1,1,384]{5,2,4,3,1,0:T(8,128)(2,1)S(1)} copy-done((bf16[2,1,384,1,1,384]{5,2,4,3,1,0:T(8,128)(2,1)S(1)}, bf16[2,1,384,1,1,384]{5,2,4,3,1,0:T(8,128)(2,1)}, u32[]{:S(2)}) %copy-start) | copy-done | bytes 589848
  1.1 78.2 %shard_map.17 = f32[2,384,384]{2,1,0:T(8,128)S(1)} custom-call(bf16[2,384,384]{2,1,0:T(8,128)(2,1)S(1)} %bitcast.3), custom_call_target="tpu_custom_call" | custom-call | tf_op jit(solution)/shard_map/pallas_call | solution.py:431
  79.3 2.2 %copy.2 = f32[2,1,384,1,1,384]{5,4,3,2,1,0:T(1,128)} copy(f32[2,1,384,1,1,384]{5,2,0,4,3,1:T(8,128)S(1)} %bitcast.2) | data formatting | bytes 2359296 | tf_op jit(solution)/shard_map/reshape | solution.py:467
Async XLA Ops:
  0.0 1.1 %copy-start = (bf16[2,1,384,1,1,384]{5,2,4,3,1,0:T(8,128)(2,1)S(1)}, bf16[2,1,384,1,1,384]{5,2,4,3,1,0:T(8,128)(2,1)}, u32[]{:S(2)}) copy-start(bf16[2,1,384,1,1,384]{5,2,4,3,1,0:T(8,128)(2,1)} %param.1) | copy-start | bytes 1769476
